TPU v7x, 512 devices: a whole 4x8x8 slice. The times are simulated.
512 devices in a mesh: row: 32 (over x, y), col: 16 (over z, core).
Axes of the slice: x: 4, y: 8, z: 8, core: 2. Of those that a mesh axis runs over, the one named last changes fastest.
Arguments:
- inverse_block: float32 [16384, 16384], P('row', 'col'), may hold values from -6 to 6
- tile_list: int32 [32], replicated, may hold values from 0 to 63, as said below
- panels: bfloat16 [3, 16384, 512], P(None, 'row'), may hold values from -0.0625 to 0.0625
- links: bfloat16 [2, 512, 512], P(None, 'col'), may hold values from -0.25 to 0.25
- diag_inverse: float32 [3, 512, 512], P(None, None, 'col'), may hold values from -6 to 6
Outputs:
- panel_inverse: float32 [3, 16384, 512], P(None, 'row', 'col')
- cross_inverse: float32 [2, 512, 512], P(None, None, 'col')
- diag_block: float32 [3, 512, 512], P(None, None, 'col')
Inputs may be any that keep to these rules, and one draw needn't show every extreme that they name: `tile_list`: 32 different tile numbers in ascending order; for each g from 0 to 16 - 1, the aligned group of tiles g * (64 // 16) to (g + 1) * (64 // 16) - 1 holds at least one of them.
All inputs are finite; a program needn't handle non-finite values.
Results may differ from a plain program's by a relative error of at most 0.0003.
Values may be sent and summed in bfloat16 or wider, within the bound.
A program may use at most 64 MiB of HBM per device.

v0:
```python
import jax
import jax.numpy as jnp
from jax import lax
from jax.sharding import Mesh
from jax.sharding import PartitionSpec as P

ORDER = 16384
TILE = 256
ROW = ("row_0", "row_1")
precise = lax.Precision.HIGHEST


def from_root(array, axes, root):
    array = jnp.where(lax.axis_index(axes) == root, array, jnp.zeros_like(array))
    for axis in axes:
        array = lax.psum(array, axis)
    return array


def laid_out(blocks, dim):
    blocks = jnp.moveaxis(blocks, 0, dim)
    shape = blocks.shape
    return blocks.reshape(*shape[:dim], shape[dim] * shape[dim + 1], *shape[dim + 2 :])


def copy_for_each(array, axis):
    copies = jnp.broadcast_to(array, (lax.axis_size(axis), *array.shape))
    return lax.all_to_all(copies, axis, split_axis=0, concat_axis=0, tiled=True)


def gathered_copies(array, axis, dim):
    return laid_out(copy_for_each(array, axis), dim)


def split_up(array, dim, peers):
    shape = array.shape
    blocks = array.reshape(*shape[:dim], peers, shape[dim] // peers, *shape[dim + 1 :])
    return jnp.moveaxis(blocks, dim, 0)


def sent_and_summed(array, axis, dim):
    blocks = split_up(array, dim, lax.axis_size(axis))
    arrived = lax.all_to_all(blocks, axis, split_axis=0, concat_axis=0, tiled=True)
    return arrived.sum(axis=0)


def of_everyone(array, axis):
    everything = copy_for_each(array, axis)
    return jnp.sum(everything, axis=0)


def rows_for(lines, peers):
    spare = -len(lines) % peers
    return jnp.pad(lines, [(0, spare)] + [(0, 0)] * (lines.ndim - 1))


def total_of(array, axes):
    own = sent_and_summed(rows_for(array, lax.axis_size(axes)), axes, 0)
    whole = gathered_copies(own, axes, 0)
    return whole[: len(array)].reshape(array.shape)


def together(arrays, axis):
    ravelled, at, gathered = (jnp.concatenate([a.reshape(-1) for a in arrays]), 0, [])
    subtotal = total_of(ravelled, axis)
    for a in arrays:
        gathered.append(subtotal[at : at + a.size].reshape(a.shape))
        at += a.size
    return tuple(gathered)


def product(left, right):
    return jnp.dot(left, right, precision=precise, preferred_element_type=jnp.float32)


def local(inverse_block, tile_list, panels, links, diag_inverse):
    rows_here = inverse_block.shape[0]
    width_here = diag_inverse.shape[2]
    ratio = lax.axis_size(ROW) // lax.axis_size("col")
    row_number = lax.axis_index(ROW)
    col_number = lax.axis_index("col")
    tile_count = ORDER // TILE
    listed = jnp.any(
        tile_list[:, None] == jnp.arange(tile_count, dtype=jnp.int32)[None, :], axis=0
    ).astype(jnp.float32)
    tiles_here = rows_here // TILE
    mine = lax.dynamic_slice_in_dim(listed, row_number * tiles_here, tiles_here)
    row_mask = jnp.broadcast_to(mine[:, None], (tiles_here, TILE)).reshape(-1)
    supernodes = panels.shape[0]
    panel_parts = []
    cross_parts = []
    diag_parts = []
    previous = None
    diag_prev = None
    for supernode in range(supernodes):
        masked_panel = panels[supernode] * row_mask[:, None].astype(jnp.bfloat16)
        pieces = []
        for source in range(ratio):
            pieces.append(from_root(masked_panel, ROW, col_number * ratio + source))
        column_factor = jnp.concatenate(pieces, axis=0).astype(jnp.float32)
        local_factor = masked_panel.astype(jnp.float32)
        partial_rows = product(inverse_block, column_factor)
        if supernode > 0:
            link_block = gathered_copies(links[supernode - 1], "col", 0).astype(jnp.float32)
            link_share = lax.dynamic_slice_in_dim(
                link_block, col_number * width_here, width_here, 1
            )
            diag_full = lax.all_gather(diag_prev, "col", axis=1, tiled=True)
            factor_share = lax.dynamic_slice_in_dim(
                local_factor, col_number * width_here, width_here, 1
            )
            cross_term = product(previous.T, factor_share)
            carried = product(diag_full, link_share)
        current = sent_and_summed(partial_rows, "col", 1)
        if supernode > 0:
            current = current + product(previous, link_share)
        current = -current * row_mask[:, None]
        if supernode + 1 < supernodes:
            current_full = lax.all_gather(current, "col", axis=1, tiled=True)
        own_term = product(local_factor.T, current)
        if supernode == 0:
            diag_now = diag_inverse[supernode] - of_everyone(own_term, ROW)
        else:
            cross_sum, rest_sum = together(
                (cross_term, own_term - product(link_block.T, cross_term)), ROW
            )
            cross_block = -(cross_sum + carried)
            diag_now = diag_inverse[supernode] - rest_sum + product(link_block.T, carried)
        if supernode > 0:
            cross_parts.append(cross_block)
        panel_parts.append(current)
        diag_parts.append(diag_now)
        if supernode + 1 < supernodes:
            previous = current_full
        diag_prev = diag_now
    return (jnp.stack(panel_parts), jnp.stack(cross_parts), jnp.stack(diag_parts))


def solution(mesh):
    split = Mesh(mesh.devices.reshape(4, 8, mesh.shape["col"]), ("row_0", "row_1", "col"))
    return jax.shard_map(
        local,
        mesh=split,
        in_specs=(
            P(ROW, "col"),
            P(),
            P(None, ROW, None),
            P(None, "col", None),
            P(None, None, "col"),
        ),
        out_specs=(P(None, ROW, "col"), P(None, None, "col"), P(None, None, "col")),
        check_vma=False,
    )
```

profile of v0, /device:TPU:8, one launch (start us, length us, event | category | flops | bytes accessed | tf_op | source)
XLA Modules:
  0.0 482.6 jit_solution(13430602291217242635)
XLA Ops:
  7.2 0.9 fusion.33
  8.3 3.0 broadcast_select_fusion.5
  11.3 0.8 copy-done.1
  12.1 1.1 broadcast_select_fusion
  13.2 91.2 %all-reduce.7.cloned.1.call-done = (bf16[512,512]{1,0:T(8,128)(2,1)}, bf16[512,512]{1,0:T(8,128)(2,1)}, bf16[512,512]{1,0:T(8,128)(2,1)}, bf16[512,512]{1,0:T(8,...) async-done(((bf16[512,512]{1,0:T(8,128)(2,1)}, bf16[512,512]{1,0:T(8,128)(2,1)}, bf16[512,512]{1,0:T(8,128)(2,1)}, bf16[512,512]{1,0:T(8,128)(2,1)}, ...) | async-done | bytes 3145744 | tf_op jit(solution)/shard_map/psum | solution.py:16
  104.4 0.6 slice_bitcast_fusion
  105.0 0.9 broadcast_in_dim.24
  105.9 7.5 %all-to-all-start.2 = ((bf16[16,32,512]{2,1,0:T(8,128)(2,1)}), bf16[16,32,512]{2,1,0:T(8,128)(2,1)S(1)}, u32[]{:S(2)}, u32[]{:S(2)}) async-start(bf16[16,32,512]{2,1,0:T(8,128)(2,1)} %broadcast_in_dim.24), calls=%async_computation.2 | async-start | bytes 1048576 | tf_op jit(solution)/shard_map/all_to_all | solution.py:28
  113.4 90.5 %all-reduce.5.cloned.1.call-done = (bf16[512,512]{1,0:T(8,128)(2,1)}, bf16[512,512]{1,0:T(8,128)(2,1)}, bf16[512,512]{1,0:T(8,128)(2,1)}, bf16[512,512]{1,0:T(8,...) async-done(((bf16[512,512]{1,0:T(8,128)(2,1)}, bf16[512,512]{1,0:T(8,128)(2,1)}, bf16[512,512]{1,0:T(8,128)(2,1)}, bf16[512,512]{1,0:T(8,128)(2,1)}, ...) | async-done | bytes 3145744 | tf_op jit(solution)/shard_map/psum | solution.py:16
  203.9 4.4 fusion.9
  208.3 7.5 %all-to-all-start = ((f32[16,512,32]{1,2,0:T(8,128)}), f32[16,512,32]{1,2,0:T(8,128)}, u32[]{:S(2)}, u32[]{:S(2)}) async-start(f32[16,512,32]{1,2,0:T(8,128)} %bitcast.114), calls=%async_computation | async-start | bytes 2097152 | tf_op jit(solution)/shard_map/all_to_all | solution.py:43
  215.9 4.4 fusion.13
  220.3 22.1 %all-to-all-done = f32[16,512,32]{1,2,0:T(8,128)} async-done(((f32[16,512,32]{1,2,0:T(8,128)}), f32[16,512,32]{1,2,0:T(8,128)}, u32[]{:S(2)}, u32[]{:S(2)}) %all-to-all-start) | async-done | bytes 1048608 | tf_op jit(solution)/shard_map/all_to_all | solution.py:43
  242.4 5.0 %all-to-all-start.1 = ((f32[16,512,32]{1,2,0:T(8,128)}), f32[16,512,32]{1,2,0:T(8,128)}, u32[]{:S(2)}, u32[]{:S(2)}) async-start(f32[16,512,32]{1,2,0:T(8,128)} %bitcast.113), calls=%async_computation.1 | async-start | bytes 2097152 | tf_op jit(solution)/shard_map/all_to_all | solution.py:43
  247.4 1.3 reduce_sum.56
  248.7 1.5 fusion.21
  250.2 23.7 %all-to-all-done.1 = f32[16,512,32]{1,2,0:T(8,128)} async-done(((f32[16,512,32]{1,2,0:T(8,128)}), f32[16,512,32]{1,2,0:T(8,128)}, u32[]{:S(2)}, u32[]{:S(2)}) %all-to-all-start.1) | async-done | bytes 1048608 | tf_op jit(solution)/shard_map/all_to_all | solution.py:43
  273.9 1.6 broadcast_in_dim.27
  275.5 7.8 %all-to-all-start.7 = ((f32[32,512,32]{1,2,0:T(8,128)}), f32[32,512,32]{1,2,0:T(8,128)}, u32[]{:S(2)}, u32[]{:S(2)}) async-start(f32[32,512,32]{1,2,0:T(8,128)} %broadcast_in_dim.27), calls=%async_computation.7 | async-start | bytes 4194304 | tf_op jit(solution)/shard_map/all_to_all | solution.py:28
  283.4 0.7 all-gather.5.cloned.1.call-update
  284.1 1.3 reduce_sum.57
  285.4 42.1 %all-gather.5.cloned.1.call-done = f32[512,512]{0,1:T(8,128)} async-done(((f32[512,32]{0,1:T(8,128)}), f32[512,512]{0,1:T(8,128)}) %all-gather.5.cloned.1.call-update) | async-done | bytes 1048592 | tf_op jit(solution)/shard_map/all_gather | solution.py:119
  327.5 1.7 fusion.3
  329.3 4.2 all-to-all-done.7
  333.4 1.7 reduce_sum.60
  335.2 1.5 bitcast_subtract_fusion.3
  336.7 2.5 fusion.25
  339.2 1.0 copy.28
  340.5 1.2 fusion.4
  342.2 0.8 copy.30
  343.0 7.9 %all-to-all-start.5 = ((f32[32,1,1024]{2,1,0:T(1,128)}), f32[32,1,1024]{2,1,0:T(1,128)S(1)}, u32[]{:S(2)}, u32[]{:S(2)}) async-start(f32[32,1,1024]{2,1,0:T(1,128)} %copy.30), calls=%async_computation.5 | async-start | bytes 262144 | tf_op jit(solution)/shard_map/all_to_all | solution.py:43
  350.9 4.4 fusion.17
  355.3 5.6 %all-to-all-done.5 = f32[32,1,1024]{2,1,0:T(1,128)S(1)} async-done(((f32[32,1,1024]{2,1,0:T(1,128)}), f32[32,1,1024]{2,1,0:T(1,128)S(1)}, u32[]{:S(2)}, u32[]{:S(2)}) %all-to-all-start.5) | async-done | bytes 131104 | tf_op jit(solution)/shard_map/all_to_all | solution.py:43
  360.9 4.3 all-to-all-start.3
  365.3 0.5 all-gather.7.cloned.1.call-update
  365.9 26.2 %all-to-all-done.3 = f32[16,512,32]{1,2,0:T(8,128)} async-done(((f32[16,512,32]{1,2,0:T(8,128)}), f32[16,512,32]{1,2,0:T(8,128)}, u32[]{:S(2)}, u32[]{:S(2)}) %all-to-all-start.3) | async-done | bytes 1048608 | tf_op jit(solution)/shard_map/all_to_all | solution.py:43
  392.2 16.4 %all_to_all.60 = f32[32,1,1024]{2,1,0:T(1,128)S(1)} all-to-all(f32[32,1,1024]{2,1,0:T(1,128)S(1)} %broadcast_in_dim.26), channel_id=1, replica_groups=mesh['row_0'=4,'row_1'=8,'col'=16] {'row_0','row_1'}, dimensions={0} | all-to-all | bytes 262144 | tf_op jit(solution)/shard_map/all_to_all | solution.py:28
  408.7 0.8 broadcast_in_dim.25
  409.5 3.6 all-to-all-start.4
  413.1 1.9 reduce_sum.58
  415.1 0.8 slice_reduce_fusion.3
  416.1 1.8 fusion.30
  417.9 1.9 fusion.6
  419.8 6.4 %all-gather.7.cloned.1.call-done = f32[512,512]{0,1:T(8,128)} async-done(((f32[512,32]{0,1:T(8,128)}), f32[512,512]{0,1:T(8,128)}) %all-gather.7.cloned.1.call-update) | async-done | bytes 1048592 | tf_op jit(solution)/shard_map/all_gather | solution.py:119
  426.2 1.9 fusion.23
  428.2 1.4 all-to-all-done.4
  429.6 1.7 fusion.1
  432.0 1.2 fusion.5
  433.4 0.8 concatenate.32
  434.3 0.9 maximum_bitcast_fusion.1
  435.2 0.8 copy.34
  436.0 9.4 %all-to-all-start.8 = ((f32[32,1,1024]{2,1,0:T(1,128)}), f32[32,1,1024]{2,1,0:T(1,128)S(1)}, u32[]{:S(2)}, u32[]{:S(2)}) async-start(f32[32,1,1024]{2,1,0:T(1,128)} %copy.34), calls=%async_computation.8 | async-start | bytes 262144 | tf_op jit(solution)/shard_map/all_to_all | solution.py:43
  445.4 0.8 bitcast_multiply_fusion.4
  446.3 1.0 reshape.132
  447.3 8.2 %all-to-all-done.8 = f32[32,1,1024]{2,1,0:T(1,128)S(1)} async-done(((f32[32,1,1024]{2,1,0:T(1,128)}), f32[32,1,1024]{2,1,0:T(1,128)S(1)}, u32[]{:S(2)}, u32[]{:S(2)}) %all-to-all-start.8) | async-done | bytes 131104 | tf_op jit(solution)/shard_map/all_to_all | solution.py:43
  455.6 0.7 broadcast_in_dim.28
  456.3 4.4 all-to-all-start.9
  460.7 0.7 pad_maximum_fusion
  461.4 0.8 bitcast_subtract_fusion.1
  462.3 8.3 %all-to-all-done.9 = f32[32,1,1024]{2,1,0:T(1,128)S(1)} async-done(((f32[32,1,1024]{2,1,0:T(1,128)}), f32[32,1,1024]{2,1,0:T(1,128)S(1)}, u32[]{:S(2)}, u32[]{:S(2)}) %all-to-all-start.9) | async-done | bytes 131104 | tf_op jit(solution)/shard_map/all_to_all | solution.py:28
  471.4 1.7 fusion.27
  473.2 1.2 fusion.8
  474.4 0.7 pad_maximum_fusion.2
  475.0 0.7 pad_maximum_fusion.1
  (70 shorter events, 3.7 us)
Async XLA Ops:
  7.2 196.7 %copy-start = (f32[512,1024]{1,0:T(8,128)S(1)}, f32[512,1024]{1,0:T(8,128)}, u32[]{:S(2)}) copy-start(f32[512,1024]{1,0:T(8,128)} %param.5) | copy-start | bytes 6291460
  7.2 97.2 %all-reduce.7.cloned.1.call-start = ((), (), s32[]{:S(2)}) async-start(), calls=%async_computation.15 | async-start | bytes 6291456 | tf_op jit(solution)/shard_map/psum | solution.py:16
  11.3 0.8 copy-start.1
  13.2 91.2 %copy-start.14 = (bf16[2,32,512]{2,1,0:T(8,128)(2,1)S(1)}, bf16[2,32,512]{2,1,0:T(8,128)(2,1)}, u32[]{:S(2)}) copy-start(bf16[2,32,512]{2,1,0:T(8,128)(2,1)} %param.8) | copy-start | bytes 196612
  13.2 190.7 %all-reduce.5.cloned.1.call-start = ((), (), s32[]{:S(2)}) async-start(), calls=%async_computation.14 | async-start | bytes 6291456 | tf_op jit(solution)/shard_map/psum | solution.py:16
  105.9 102.4 %all-to-all-start.2 = ((bf16[16,32,512]{2,1,0:T(8,128)(2,1)}), bf16[16,32,512]{2,1,0:T(8,128)(2,1)S(1)}, u32[]{:S(2)}, u32[]{:S(2)}) async-start(bf16[16,32,512]{2,1,0:T(8,128)(2,1)} %broadcast_in_dim.24), calls=%async_computation.2 | async-start | bytes 1048576 | tf_op jit(solution)/shard_map/all_to_all | solution.py:28
  208.3 34.1 %all-to-all-start = ((f32[16,512,32]{1,2,0:T(8,128)}), f32[16,512,32]{1,2,0:T(8,128)}, u32[]{:S(2)}, u32[]{:S(2)}) async-start(f32[16,512,32]{1,2,0:T(8,128)} %bitcast.114), calls=%async_computation | async-start | bytes 2097152 | tf_op jit(solution)/shard_map/all_to_all | solution.py:43
  242.4 31.5 %all-to-all-start.1 = ((f32[16,512,32]{1,2,0:T(8,128)}), f32[16,512,32]{1,2,0:T(8,128)}, u32[]{:S(2)}, u32[]{:S(2)}) async-start(f32[16,512,32]{1,2,0:T(8,128)} %bitcast.113), calls=%async_computation.1 | async-start | bytes 2097152 | tf_op jit(solution)/shard_map/all_to_all | solution.py:43
  248.7 26.8 %copy-start.7 = (f32[512,32]{0,1:T(8,128)}, f32[512,32]{0,1:T(8,128)S(1)}, u32[]{:S(2)}) copy-start(f32[512,32]{0,1:T(8,128)S(1)} %reduce_sum.56) | copy-start | bytes 196612
  248.7 26.8 %copy-start.12 = (f32[512,32]{0,1:T(8,128)}, f32[512,32]{0,1:T(8,128)S(1)}, u32[]{:S(2)}) copy-start(f32[512,32]{0,1:T(8,128)S(1)} %negate_multiply_fusion) | copy-start | bytes 196612
  275.5 57.9 %all-to-all-start.7 = ((f32[32,512,32]{1,2,0:T(8,128)}), f32[32,512,32]{1,2,0:T(8,128)}, u32[]{:S(2)}, u32[]{:S(2)}) async-start(f32[32,512,32]{1,2,0:T(8,128)} %broadcast_in_dim.27), calls=%async_computation.7 | async-start | bytes 4194304 | tf_op jit(solution)/shard_map/all_to_all | solution.py:28
  283.3 44.2 %all-gather.5.cloned.1.call-start = ((), (), s32[]{:S(2)}) async-start(), calls=%async_computation.10 | async-start | bytes 1114112 | tf_op jit(solution)/shard_map/all_gather | solution.py:119
  284.1 132.1 %all-gather.9.cloned.1.call-start = ((), (), s32[]{:S(2)}) async-start(), calls=%async_computation.12 | async-start | bytes 1114112 | tf_op jit(solution)/shard_map/all_gather | solution.py:108
  329.2 11.3 %copy-start.3 = (f32[512,32]{0,1:T(8,128)}, f32[512,32]{0,1:T(8,128)S(1)}, u32[]{:S(2)}) copy-start(f32[512,32]{0,1:T(8,128)S(1)} %fusion.3) | copy-start | bytes 196612
  343.0 17.9 %all-to-all-start.5 = ((f32[32,1,1024]{2,1,0:T(1,128)}), f32[32,1,1024]{2,1,0:T(1,128)S(1)}, u32[]{:S(2)}, u32[]{:S(2)}) async-start(f32[32,1,1024]{2,1,0:T(1,128)} %copy.30), calls=%async_computation.5 | async-start | bytes 262144 | tf_op jit(solution)/shard_map/all_to_all | solution.py:43
  355.3 53.3 %copy-start.13 = (bf16[32,512]{1,0:T(8,128)(2,1)S(1)}, bf16[32,512]{1,0:T(8,128)(2,1)}, u32[]{:S(2)}) copy-start(bf16[32,512]{1,0:T(8,128)(2,1)} %get-tuple-element.29) | copy-start | bytes 98308
  360.9 31.2 %all-to-all-start.3 = ((f32[16,512,32]{1,2,0:T(8,128)}), f32[16,512,32]{1,2,0:T(8,128)}, u32[]{:S(2)}, u32[]{:S(2)}) async-start(f32[16,512,32]{1,2,0:T(8,128)} %bitcast.112), calls=%async_computation.3 | async-start | bytes 2097152 | tf_op jit(solution)/shard_map/all_to_all | solution.py:43
  365.2 60.9 %all-gather.7.cloned.1.call-start = ((), (), s32[]{:S(2)}) async-start(), calls=%async_computation.11 | async-start | bytes 1114112 | tf_op jit(solution)/shard_map/all_gather | solution.py:119
  409.5 20.1 %all-to-all-start.4 = ((bf16[16,32,512]{2,1,0:T(8,128)(2,1)}), bf16[16,32,512]{2,1,0:T(8,128)(2,1)S(1)}, u32[]{:S(2)}, u32[]{:S(2)}) async-start(bf16[16,32,512]{2,1,0:T(8,128)(2,1)} %broadcast_in_dim.25), calls=%async_computation.4 | async-start | bytes 1048576 | tf_op jit(solution)/shard_map/all_to_all | solution.py:28
  413.1 58.3 %all-gather.11.cloned.1.call-start = ((), (), s32[]{:S(2)}) async-start(), calls=%async_computation.13 | async-start | bytes 1114112 | tf_op jit(solution)/shard_map/all_gather | solution.py:108
  417.9 8.3 %copy-start.5 = (f32[512,32]{0,1:T(8,128)}, f32[512,32]{0,1:T(8,128)S(1)}, u32[]{:S(2)}) copy-start(f32[512,32]{0,1:T(8,128)S(1)} %fusion.30) | copy-start | bytes 196612
  419.7 11.7 %copy-start.2 = (bf16[512,512]{1,0:T(8,128)(2,1)S(1)}, bf16[512,512]{1,0:T(8,128)(2,1)}, u32[]{:S(2)}) copy-start(bf16[512,512]{1,0:T(8,128)(2,1)} %copy-done.1) | copy-start | bytes 1572868
  428.1 1.6 copy-start.11
  431.4 0.6 copy-start.8
  431.4 29.3 %copy-start.4 = (f32[512,32]{0,1:T(8,128)S(1)}, f32[512,32]{0,1:T(8,128)}, u32[]{:S(2)}) copy-start(f32[512,32]{0,1:T(8,128)} %copy-done.3) | copy-start | bytes 196612
  433.3 27.4 %copy-start.9 = (f32[512,32]{0,1:T(8,128)S(1)}, f32[512,32]{0,1:T(8,128)}, u32[]{:S(2)}) copy-start(f32[512,32]{0,1:T(8,128)} %copy-done.8) | copy-start | bytes 196612
  434.3 37.0 %copy-start.6 = (f32[512,32]{0,1:T(8,128)S(1)}, f32[512,32]{0,1:T(8,128)}, u32[]{:S(2)}) copy-start(f32[512,32]{0,1:T(8,128)} %copy-done.5) | copy-start | bytes 196612
  436.0 19.5 %all-to-all-start.8 = ((f32[32,1,1024]{2,1,0:T(1,128)}), f32[32,1,1024]{2,1,0:T(1,128)S(1)}, u32[]{:S(2)}, u32[]{:S(2)}) async-start(f32[32,1,1024]{2,1,0:T(1,128)} %copy.34), calls=%async_computation.8 | async-start | bytes 262144 | tf_op jit(solution)/shard_map/all_to_all | solution.py:43
  456.3 14.2 %all-to-all-start.9 = ((f32[32,1,1024]{2,1,0:T(1,128)}), f32[32,1,1024]{2,1,0:T(1,128)S(1)}, u32[]{:S(2)}, u32[]{:S(2)}) async-start(f32[32,1,1024]{2,1,0:T(1,128)} %broadcast_in_dim.28), calls=%async_computation.9 | async-start | bytes 262144 | tf_op jit(solution)/shard_map/all_to_all | solution.py:28
  462.3 12.8 %copy-start.10 = (f32[512,32]{0,1:T(8,128)S(1)}, f32[512,32]{0,1:T(8,128)}, u32[]{:S(2)}) copy-start(f32[512,32]{0,1:T(8,128)} %fusion.6) | copy-start | bytes 196612
Sparse Core Ops, SparseCore 0:
  13.3 91.0 all-reduce.6
  107.1 96.7 all-reduce.4
  286.8 40.6 all-gather.4
  336.8 38.3 all-gather.8
  377.7 48.4 all-gather.6
  428.1 40.9 all-gather.10
where the time goes:
time: 484 us; the launch traced here: 483 us
  waiting for transfers between devices  331 us (68%)
  starting transfers between devices  57.7 us (12%)
  matrix products  32.3 us (7%)
  other arithmetic  17.6 us (4%)
  blocking collectives  16.4 us (3%)
  between operations  14.5 us (3%)
  local copies, waits for them, and re-layouts  12.9 us (3%)
    psum x2, waiting for transfers between devices, from_root(): array = lax.psum(array, axis)  182 us
    all_to_all x5, waiting for transfers between devices, sent_and_summed(): lax.all_to_all(blocks, axis, split_axis=0, concat_axis=0, tiled=True)  85.8 us
    all_gather x2, waiting for transfers between devices, local(): current_full = lax.all_gather(current, 'col', axis=1, tiled=True)  48.5 us
    all_to_all x5, starting transfers between devices, sent_and_summed(): lax.all_to_all(blocks, axis, split_axis=0, concat_axis=0, tiled=True)  34.2 us
    dot_general x16, matrix products, product(): jnp.dot(left, right, precision=precise, preferred_element_type=jnp.float32)  32.3 us
    all_to_all x4, starting transfers between devices, copy_for_each(): return lax.all_to_all(copies, axis, split_axis=0, concat_axis=0, tiled=True)  23.2 us
    all_to_all x1, blocking collectives, copy_for_each(): return lax.all_to_all(copies, axis, split_axis=0, concat_axis=0, tiled=True)  16.4 us
    all_to_all x4, waiting for transfers between devices, copy_for_each(): return lax.all_to_all(copies, axis, split_axis=0, concat_axis=0, tiled=True)  13.9 us
  transfers between devices with their start and end apart: 15, of which 12 were waited for; matrix products, arithmetic and copies ran while one was open for 10% of the time, Pallas kernels for 0%

commit v1 on v0

--- a/solution.py
+++ b/solution.py
@@ -3,6 +3,7 @@
 from jax import lax
 from jax.sharding import Mesh
 from jax.sharding import PartitionSpec as P
+from jax.lax import all_gather
 
 ORDER = 16384
 TILE = 256
@@ -13,7 +14,7 @@
 def from_root(array, axes, root):
     array = jnp.where(lax.axis_index(axes) == root, array, jnp.zeros_like(array))
     for axis in axes:
-        array = lax.psum(array, axis)
+        array = jnp.sum(all_gather(array, axis), 0)
     return array
 
 

time: 484 us -> 819 us (1.69)
  waiting for transfers between devices: 331 us -> 620 us
  other arithmetic: 17.6 us -> 58.2 us
    all_gather x0 -> x12, waiting for transfers between devices: none -> 496 us  [from_root(): array = jnp.sum(all_gather(array, axis), 0)]
    psum x2 -> x0, waiting for transfers between devices: 182 us -> none  [from_root(): array = lax.psum(array, axis)]
    reduce_sum x0 -> x12, other arithmetic: none -> 38.3 us  [from_root(): array = jnp.sum(all_gather(array, axis), 0)]
    all_to_all x5, waiting for transfers between devices: 85.8 us -> 64.1 us  [sent_and_summed(): lax.all_to_all(blocks, axis, split_axis=0, concat_axis=0, tiled=True)]
    all_gather x2, waiting for transfers between devices: 48.5 us -> 40 us  [local(): current_full = lax.all_gather(current, 'col', axis=1, tiled=True)]
  transfers between devices with their start and end apart: 15 -> 25, of which waited for: 12 -> 19; matrix products, arithmetic and copies ran while one was open for 10% -> 12% of each run, Pallas kernels for 0% -> 0%
where the time goes in v1:
time: 819 us; the launch traced here: 816 us
  waiting for transfers between devices  620 us (76%)
  starting transfers between devices  59.6 us (7%)
  other arithmetic  58.2 us (7%)
  matrix products  32.7 us (4%)
  blocking collectives  15.6 us (2%)
  local copies, waits for them, and re-layouts  15.3 us (2%)
  between operations  14.4 us (2%)
    all_gather x12, waiting for transfers between devices, from_root(): array = jnp.sum(all_gather(array, axis), 0)  496 us
    all_to_all x5, waiting for transfers between devices, sent_and_summed(): lax.all_to_all(blocks, axis, split_axis=0, concat_axis=0, tiled=True)  64.1 us
    all_gather x2, waiting for transfers between devices, local(): current_full = lax.all_gather(current, 'col', axis=1, tiled=True)  40 us
    reduce_sum x12, other arithmetic, from_root(): array = jnp.sum(all_gather(array, axis), 0)  38.3 us
    all_to_all x5, starting transfers between devices, sent_and_summed(): lax.all_to_all(blocks, axis, split_axis=0, concat_axis=0, tiled=True)  34.1 us
    dot_general x16, matrix products, product(): jnp.dot(left, right, precision=precise, preferred_element_type=jnp.float32)  32.7 us
    all_to_all x4, starting transfers between devices, copy_for_each(): return lax.all_to_all(copies, axis, split_axis=0, concat_axis=0, tiled=True)  24.9 us
  transfers between devices with their start and end apart: 25, of which 19 were waited for; matrix products, arithmetic and copies ran while one was open for 12% of the time, Pallas kernels for 0%

profile of v1, /device:TPU:8, one launch (start us, length us, event | category | flops | bytes accessed | tf_op | source)
XLA Modules:
  0.0 816.1 jit_solution(10404926164793665126)
XLA Ops:
  8.3 3.4 broadcast_select_fusion.5
  14.9 37.5 %all-gather.25.cloned.1.call-done = bf16[4,512,512]{2,1,0:T(8,128)(2,1)} async-done(((bf16[1,512,512]{2,1,0:T(8,128)(2,1)}), bf16[4,512,512]{2,1,0:T(8,128)(2,1)}) %all-gather.25.cloned.1.call-update) | async-done | bytes 2097168 | tf_op jit(solution)/shard_map/all_gather | solution.py:17
  52.5 2.9 reduce_sum.202
  55.4 35.4 %all-gather.23.cloned.1.call-done = bf16[4,512,512]{2,1,0:T(8,128)(2,1)} async-done(((bf16[1,512,512]{2,1,0:T(8,128)(2,1)}), bf16[4,512,512]{2,1,0:T(8,128)(2,1)}) %all-gather.23.cloned.1.call-update) | async-done | bytes 2097168 | tf_op jit(solution)/shard_map/all_gather | solution.py:17
  90.8 2.9 reduce_sum.200
  93.7 35.4 %all-gather.29.cloned.1.call-done = bf16[4,512,512]{2,1,0:T(8,128)(2,1)} async-done(((bf16[1,512,512]{2,1,0:T(8,128)(2,1)}), bf16[4,512,512]{2,1,0:T(8,128)(2,1)}) %all-gather.29.cloned.1.call-update) | async-done | bytes 2097168 | tf_op jit(solution)/shard_map/all_gather | solution.py:17
  129.1 2.9 reduce_sum.207
  132.1 35.2 %all-gather.27.cloned.1.call-done = bf16[4,512,512]{2,1,0:T(8,128)(2,1)} async-done(((bf16[1,512,512]{2,1,0:T(8,128)(2,1)}), bf16[4,512,512]{2,1,0:T(8,128)(2,1)}) %all-gather.27.cloned.1.call-update) | async-done | bytes 2097168 | tf_op jit(solution)/shard_map/all_gather | solution.py:17
  167.3 2.9 reduce_sum.205
  170.2 35.2 %all-gather.35.cloned.1.call-done = bf16[4,512,512]{2,1,0:T(8,128)(2,1)} async-done(((bf16[1,512,512]{2,1,0:T(8,128)(2,1)}), bf16[4,512,512]{2,1,0:T(8,128)(2,1)}) %all-gather.35.cloned.1.call-update) | async-done | bytes 2097168 | tf_op jit(solution)/shard_map/all_gather | solution.py:17
  205.4 2.9 reduce_sum.212
  208.4 35.2 %all-gather.33.cloned.1.call-done = bf16[4,512,512]{2,1,0:T(8,128)(2,1)} async-done(((bf16[1,512,512]{2,1,0:T(8,128)(2,1)}), bf16[4,512,512]{2,1,0:T(8,128)(2,1)}) %all-gather.33.cloned.1.call-update) | async-done | bytes 2097168 | tf_op jit(solution)/shard_map/all_gather | solution.py:17
  243.6 2.9 reduce_sum.210
  248.0 7.5 all-to-all-start.2
  255.5 46.0 %all-gather.45.cloned.1.call-done = bf16[4096,512]{1,0:T(8,128)(2,1)} async-done(((bf16[512,512]{1,0:T(8,128)(2,1)}), bf16[4096,512]{1,0:T(8,128)(2,1)}) %all-gather.45.cloned.1.call-update) | async-done | bytes 4194320 | tf_op jit(solution)/shard_map/all_gather | solution.py:17
  301.5 3.1 reduce_sum.203
  304.5 55.2 %all-gather.43.cloned.1.call-done = bf16[4096,512]{1,0:T(8,128)(2,1)} async-done(((bf16[512,512]{1,0:T(8,128)(2,1)}), bf16[4096,512]{1,0:T(8,128)(2,1)}) %all-gather.43.cloned.1.call-update) | async-done | bytes 4194320 | tf_op jit(solution)/shard_map/all_gather | solution.py:17
  359.7 3.8 reduce_sum.201
  363.4 4.3 fusion.9
  367.8 7.5 all-to-all-start
  375.3 42.6 %all-gather.49.cloned.1.call-done = bf16[4096,512]{1,0:T(8,128)(2,1)} async-done(((bf16[512,512]{1,0:T(8,128)(2,1)}), bf16[4096,512]{1,0:T(8,128)(2,1)}) %all-gather.49.cloned.1.call-update) | async-done | bytes 4194320 | tf_op jit(solution)/shard_map/all_gather | solution.py:17
  417.9 3.1 reduce_sum.208
  421.0 55.0 %all-gather.47.cloned.1.call-done = bf16[4096,512]{1,0:T(8,128)(2,1)} async-done(((bf16[512,512]{1,0:T(8,128)(2,1)}), bf16[4096,512]{1,0:T(8,128)(2,1)}) %all-gather.47.cloned.1.call-update) | async-done | bytes 4194320 | tf_op jit(solution)/shard_map/all_gather | solution.py:17
  476.0 3.7 reduce_sum.206
  479.7 4.3 fusion.13
  484.0 7.5 all-to-all-start.1
  491.6 1.3 reduce_sum.204
  492.9 1.5 fusion.21
  494.4 23.7 %all-to-all-done.1 = f32[16,512,32]{1,2,0:T(8,128)} async-done(((f32[16,512,32]{1,2,0:T(8,128)}), f32[16,512,32]{1,2,0:T(8,128)}, u32[]{:S(2)}, u32[]{:S(2)}) %all-to-all-start.1) | async-done | bytes 1048608 | tf_op jit(solution)/shard_map/all_to_all | solution.py:44
  518.1 1.6 broadcast_in_dim.27
  519.7 9.0 %all-to-all-start.7 = ((f32[32,512,32]{1,2,0:T(8,128)}), f32[32,512,32]{1,2,0:T(8,128)}, u32[]{:S(2)}, u32[]{:S(2)}) async-start(f32[32,512,32]{1,2,0:T(8,128)} %broadcast_in_dim.27), calls=%async_computation.7 | async-start | bytes 4194304 | tf_op jit(solution)/shard_map/all_to_all | solution.py:29
  529.6 2.1 bitcast_multiply_fusion.3
  531.7 7.8 all-gather.53.cloned.1.call-done
  539.5 3.8 reduce_sum.213
  543.3 75.2 %all-gather.51.cloned.1.call-done = bf16[4096,512]{1,0:T(8,128)(2,1)} async-done(((bf16[512,512]{1,0:T(8,128)(2,1)}), bf16[4096,512]{1,0:T(8,128)(2,1)}) %all-gather.51.cloned.1.call-update) | async-done | bytes 4194320 | tf_op jit(solution)/shard_map/all_gather | solution.py:17
  618.5 3.8 reduce_sum.211
  622.2 1.3 reduce_sum.209
  623.5 40.0 %all-gather.31.cloned.1.call-done = f32[512,512]{0,1:T(8,128)} async-done(((f32[512,32]{0,1:T(8,128)}), f32[512,512]{0,1:T(8,128)}) %all-gather.31.cloned.1.call-update) | async-done | bytes 1048592 | tf_op jit(solution)/shard_map/all_gather | solution.py:120
  663.5 1.7 fusion.3
  665.3 1.8 reduce_sum.216
  667.1 1.5 bitcast_subtract_fusion.3
  668.6 2.5 fusion.26
  672.4 1.9 fusion.4
  674.3 1.7 copy.29
  679.5 9.8 %all-to-all-start.5 = ((f32[32,1,1024]{2,1,0:T(1,128)}), f32[32,1,1024]{2,1,0:T(1,128)S(1)}, u32[]{:S(2)}, u32[]{:S(2)}) async-start(f32[32,1,1024]{2,1,0:T(1,128)} %copy.30), calls=%async_computation.5 | async-start | bytes 262144 | tf_op jit(solution)/shard_map/all_to_all | solution.py:44
  689.4 4.3 fusion.17
  693.7 5.8 all-to-all-done.5
  699.4 4.6 all-to-all-start.3
  704.7 25.9 %all-to-all-done.3 = f32[16,512,32]{1,2,0:T(8,128)} async-done(((f32[16,512,32]{1,2,0:T(8,128)}), f32[16,512,32]{1,2,0:T(8,128)}, u32[]{:S(2)}, u32[]{:S(2)}) %all-to-all-start.3) | async-done | bytes 1048608 | tf_op jit(solution)/shard_map/all_to_all | solution.py:44
  730.7 15.6 %all_to_all.60 = f32[32,1,1024]{2,1,0:T(1,128)S(1)} all-to-all(f32[32,1,1024]{2,1,0:T(1,128)S(1)} %broadcast_in_dim.26), channel_id=1, replica_groups=mesh['row_0'=4,'row_1'=8,'col'=16] {'row_0','row_1'}, dimensions={0} | all-to-all | bytes 262144 | tf_op jit(solution)/shard_map/all_to_all | solution.py:29
  747.1 3.8 all-to-all-start.4
  751.0 1.9 reduce_sum.214
  754.0 1.7 fusion.31
  755.8 1.8 fusion.6
  757.7 1.9 fusion.24
  759.8 7.1 all-to-all-done.4
  766.9 1.7 fusion.1
  769.3 1.2 fusion.5
  773.3 4.6 all-to-all-start.8
  779.8 8.7 %all-to-all-done.8 = f32[32,1,1024]{2,1,0:T(1,128)S(1)} async-done(((f32[32,1,1024]{2,1,0:T(1,128)}), f32[32,1,1024]{2,1,0:T(1,128)S(1)}, u32[]{:S(2)}, u32[]{:S(2)}) %all-to-all-start.8) | async-done | bytes 131104 | tf_op jit(solution)/shard_map/all_to_all | solution.py:44
  789.4 4.5 all-to-all-start.9
  795.5 8.9 %all-to-all-done.9 = f32[32,1,1024]{2,1,0:T(1,128)S(1)} async-done(((f32[32,1,1024]{2,1,0:T(1,128)}), f32[32,1,1024]{2,1,0:T(1,128)S(1)}, u32[]{:S(2)}, u32[]{:S(2)}) %all-to-all-start.9) | async-done | bytes 131104 | tf_op jit(solution)/shard_map/all_to_all | solution.py:29
  805.2 1.7 fusion.28
  807.0 1.2 fusion.8
  (112 shorter events, 24.4 us)
Async XLA Ops:
  7.2 356.3 %copy-start = (f32[512,1024]{1,0:T(8,128)S(1)}, f32[512,1024]{1,0:T(8,128)}, u32[]{:S(2)}) copy-start(f32[512,1024]{1,0:T(8,128)} %param.5) | copy-start | bytes 6291460
  7.2 45.3 %all-gather.25.cloned.1.call-start = ((), (), s32[]{:S(2)}) async-start(), calls=%async_computation.11 | async-start | bytes 2621440 | tf_op jit(solution)/shard_map/all_gather | solution.py:17
  11.7 79.1 %all-gather.23.cloned.1.call-start = ((), (), s32[]{:S(2)}) async-start(), calls=%async_computation.10 | async-start | bytes 2621440 | tf_op jit(solution)/shard_map/all_gather | solution.py:17
  12.4 116.7 %all-gather.29.cloned.1.call-start = ((), (), s32[]{:S(2)}) async-start(), calls=%async_computation.13 | async-start | bytes 2621440 | tf_op jit(solution)/shard_map/all_gather | solution.py:17
  13.2 154.1 %all-gather.27.cloned.1.call-start = ((), (), s32[]{:S(2)}) async-start(), calls=%async_computation.12 | async-start | bytes 2621440 | tf_op jit(solution)/shard_map/all_gather | solution.py:17
  13.7 191.7 %all-gather.35.cloned.1.call-start = ((), (), s32[]{:S(2)}) async-start(), calls=%async_computation.16 | async-start | bytes 2621440 | tf_op jit(solution)/shard_map/all_gather | solution.py:17
  14.3 229.3 %all-gather.33.cloned.1.call-start = ((), (), s32[]{:S(2)}) async-start(), calls=%async_computation.15 | async-start | bytes 2621440 | tf_op jit(solution)/shard_map/all_gather | solution.py:17
  14.9 286.6 %all-gather.45.cloned.1.call-start = ((), (), s32[]{:S(2)}) async-start(), calls=%async_computation.21 | async-start | bytes 4718592 | tf_op jit(solution)/shard_map/all_gather | solution.py:17
  55.4 304.3 %all-gather.43.cloned.1.call-start = ((), (), s32[]{:S(2)}) async-start(), calls=%async_computation.20 | async-start | bytes 4718592 | tf_op jit(solution)/shard_map/all_gather | solution.py:17
  93.7 324.2 %all-gather.49.cloned.1.call-start = ((), (), s32[]{:S(2)}) async-start(), calls=%async_computation.23 | async-start | bytes 4718592 | tf_op jit(solution)/shard_map/all_gather | solution.py:17
  132.0 344.0 %all-gather.47.cloned.1.call-start = ((), (), s32[]{:S(2)}) async-start(), calls=%async_computation.22 | async-start | bytes 4718592 | tf_op jit(solution)/shard_map/all_gather | solution.py:17
  170.2 369.4 %all-gather.53.cloned.1.call-start = ((), (), s32[]{:S(2)}) async-start(), calls=%async_computation.25 | async-start | bytes 4718592 | tf_op jit(solution)/shard_map/all_gather | solution.py:17
  208.3 38.2 %copy-start.14 = (bf16[2,32,512]{2,1,0:T(8,128)(2,1)S(1)}, bf16[2,32,512]{2,1,0:T(8,128)(2,1)}, u32[]{:S(2)}) copy-start(bf16[2,32,512]{2,1,0:T(8,128)(2,1)} %param.8) | copy-start | bytes 196612
  208.4 410.1 %all-gather.51.cloned.1.call-start = ((), (), s32[]{:S(2)}) async-start(), calls=%async_computation.24 | async-start | bytes 4718592 | tf_op jit(solution)/shard_map/all_gather | solution.py:17
  248.0 119.8 %all-to-all-start.2 = ((bf16[16,32,512]{2,1,0:T(8,128)(2,1)}), bf16[16,32,512]{2,1,0:T(8,128)(2,1)S(1)}, u32[]{:S(2)}, u32[]{:S(2)}) async-start(bf16[16,32,512]{2,1,0:T(8,128)(2,1)} %broadcast_in_dim.24), calls=%async_computation.2 | async-start | bytes 1048576 | tf_op jit(solution)/shard_map/all_to_all | solution.py:29
  367.8 116.3 %all-to-all-start = ((f32[16,512,32]{1,2,0:T(8,128)}), f32[16,512,32]{1,2,0:T(8,128)}, u32[]{:S(2)}, u32[]{:S(2)}) async-start(f32[16,512,32]{1,2,0:T(8,128)} %bitcast.118), calls=%async_computation | async-start | bytes 2097152 | tf_op jit(solution)/shard_map/all_to_all | solution.py:44
  484.0 34.1 %all-to-all-start.1 = ((f32[16,512,32]{1,2,0:T(8,128)}), f32[16,512,32]{1,2,0:T(8,128)}, u32[]{:S(2)}, u32[]{:S(2)}) async-start(f32[16,512,32]{1,2,0:T(8,128)} %bitcast.120), calls=%async_computation.1 | async-start | bytes 2097152 | tf_op jit(solution)/shard_map/all_to_all | solution.py:44
  492.9 26.8 %copy-start.7 = (f32[512,32]{0,1:T(8,128)}, f32[512,32]{0,1:T(8,128)S(1)}, u32[]{:S(2)}) copy-start(f32[512,32]{0,1:T(8,128)S(1)} %reduce_sum.204) | copy-start | bytes 196612
  492.9 26.8 %copy-start.12 = (f32[512,32]{0,1:T(8,128)}, f32[512,32]{0,1:T(8,128)S(1)}, u32[]{:S(2)}) copy-start(f32[512,32]{0,1:T(8,128)S(1)} %negate_multiply_fusion) | copy-start | bytes 196612
  519.7 145.6 %all-to-all-start.7 = ((f32[32,512,32]{1,2,0:T(8,128)}), f32[32,512,32]{1,2,0:T(8,128)}, u32[]{:S(2)}, u32[]{:S(2)}) async-start(f32[32,512,32]{1,2,0:T(8,128)} %broadcast_in_dim.27), calls=%async_computation.7 | async-start | bytes 4194304 | tf_op jit(solution)/shard_map/all_to_all | solution.py:29
  528.8 134.8 %all-gather.31.cloned.1.call-start = ((), (), s32[]{:S(2)}) async-start(), calls=%async_computation.14 | async-start | bytes 1114112 | tf_op jit(solution)/shard_map/all_gather | solution.py:120
  529.5 224.5 %all-gather.39.cloned.1.call-start = ((), (), s32[]{:S(2)}) async-start(), calls=%async_computation.18 | async-start | bytes 1114112 | tf_op jit(solution)/shard_map/all_gather | solution.py:109
  665.3 7.1 copy-start.3
  672.4 16.9 %copy-start.2 = (bf16[512,512]{1,0:T(8,128)(2,1)S(1)}, bf16[512,512]{1,0:T(8,128)(2,1)}, u32[]{:S(2)}) copy-start(bf16[512,512]{1,0:T(8,128)(2,1)} %reduce_sum.213) | copy-start | bytes 1572868
  679.5 19.9 %all-to-all-start.5 = ((f32[32,1,1024]{2,1,0:T(1,128)}), f32[32,1,1024]{2,1,0:T(1,128)S(1)}, u32[]{:S(2)}, u32[]{:S(2)}) async-start(f32[32,1,1024]{2,1,0:T(1,128)} %copy.30), calls=%async_computation.5 | async-start | bytes 262144 | tf_op jit(solution)/shard_map/all_to_all | solution.py:44
  693.7 52.6 %copy-start.13 = (bf16[32,512]{1,0:T(8,128)(2,1)S(1)}, bf16[32,512]{1,0:T(8,128)(2,1)}, u32[]{:S(2)}) copy-start(bf16[32,512]{1,0:T(8,128)(2,1)} %get-tuple-element.15) | copy-start | bytes 98308
  699.4 31.1 %all-to-all-start.3 = ((f32[16,512,32]{1,2,0:T(8,128)}), f32[16,512,32]{1,2,0:T(8,128)}, u32[]{:S(2)}, u32[]{:S(2)}) async-start(f32[16,512,32]{1,2,0:T(8,128)} %bitcast.119), calls=%async_computation.3 | async-start | bytes 2097152 | tf_op jit(solution)/shard_map/all_to_all | solution.py:44
  704.0 53.7 %all-gather.37.cloned.1.call-start = ((), (), s32[]{:S(2)}) async-start(), calls=%async_computation.17 | async-start | bytes 1114112 | tf_op jit(solution)/shard_map/all_gather | solution.py:120
  747.1 19.8 %all-to-all-start.4 = ((bf16[16,32,512]{2,1,0:T(8,128)(2,1)}), bf16[16,32,512]{2,1,0:T(8,128)(2,1)S(1)}, u32[]{:S(2)}, u32[]{:S(2)}) async-start(bf16[16,32,512]{2,1,0:T(8,128)(2,1)} %broadcast_in_dim.25), calls=%async_computation.4 | async-start | bytes 1048576 | tf_op jit(solution)/shard_map/all_to_all | solution.py:29
  751.0 54.2 %all-gather.41.cloned.1.call-start = ((), (), s32[]{:S(2)}) async-start(), calls=%async_computation.19 | async-start | bytes 1114112 | tf_op jit(solution)/shard_map/all_gather | solution.py:109
  755.8 1.9 copy-start.5
  757.6 11.0 %copy-start.1 = (bf16[512,512]{1,0:T(8,128)(2,1)S(1)}, bf16[512,512]{1,0:T(8,128)(2,1)}, u32[]{:S(2)}) copy-start(bf16[512,512]{1,0:T(8,128)(2,1)} %get-tuple-element.8) | copy-start | bytes 1572868
  759.6 7.3 copy-start.11
  768.7 0.6 copy-start.8
  768.7 25.2 %copy-start.4 = (f32[512,32]{0,1:T(8,128)S(1)}, f32[512,32]{0,1:T(8,128)}, u32[]{:S(2)}) copy-start(f32[512,32]{0,1:T(8,128)} %copy-done.3) | copy-start | bytes 196612
  770.5 23.4 %copy-start.9 = (f32[512,32]{0,1:T(8,128)S(1)}, f32[512,32]{0,1:T(8,128)}, u32[]{:S(2)}) copy-start(f32[512,32]{0,1:T(8,128)} %copy-done.8) | copy-start | bytes 196612
  771.6 33.6 %copy-start.6 = (f32[512,32]{0,1:T(8,128)S(1)}, f32[512,32]{0,1:T(8,128)}, u32[]{:S(2)}) copy-start(f32[512,32]{0,1:T(8,128)} %copy-done.5) | copy-start | bytes 196612
  773.3 15.3 %all-to-all-start.8 = ((f32[32,1,1024]{2,1,0:T(1,128)}), f32[32,1,1024]{2,1,0:T(1,128)S(1)}, u32[]{:S(2)}, u32[]{:S(2)}) async-start(f32[32,1,1024]{2,1,0:T(1,128)} %copy.34), calls=%async_computation.8 | async-start | bytes 262144 | tf_op jit(solution)/shard_map/all_to_all | solution.py:44
  789.4 15.0 %all-to-all-start.9 = ((f32[32,1,1024]{2,1,0:T(1,128)}), f32[32,1,1024]{2,1,0:T(1,128)S(1)}, u32[]{:S(2)}, u32[]{:S(2)}) async-start(f32[32,1,1024]{2,1,0:T(1,128)} %broadcast_in_dim.28), calls=%async_computation.9 | async-start | bytes 262144 | tf_op jit(solution)/shard_map/all_to_all | solution.py:29
  795.5 13.4 %copy-start.10 = (f32[512,32]{0,1:T(8,128)S(1)}, f32[512,32]{0,1:T(8,128)}, u32[]{:S(2)}) copy-start(f32[512,32]{0,1:T(8,128)} %fusion.6) | copy-start | bytes 196612
Sparse Core Ops, SparseCore 0:
  11.8 40.6 all-gather.24
  54.6 36.1 all-gather.22
  92.9 36.1 all-gather.28
  131.1 36.1 all-gather.26
  169.2 36.1 all-gather.34
  207.4 36.1 all-gather.32
  245.7 55.7 all-gather.44
  303.6 56.0 all-gather.42
  361.8 56.0 all-gather.48
  419.8 56.0 all-gather.46
  478.1 61.4 all-gather.52
  541.5 76.9 all-gather.50
  621.2 42.3 all-gather.30
  668.7 39.9 all-gather.38
  711.2 42.7 all-gather.36
  757.8 38.9 all-gather.40
